TPU v7x, 32 devices: a whole 2x2x4 slice. The times are simulated.
32 devices in a mesh: mod: 4 (over x, core), shard: 8 (over z, y).
Axes of the slice: x: 2, y: 2, z: 4, core: 2. Of those that a mesh axis runs over, the one named last changes fastest.
Arguments:
- tokens_b: bfloat16 [512, 4096], P(('mod', 'shard')), may hold values from -6 to 6
- labels_b: int32 [512, 1], P(('mod', 'shard')), may hold values from 0 to 3; in each aligned block of 16 rows (0 to 15, 16 to 31, ...) at most 6 rows name the same one
- tokens_a: bfloat16 [512, 4096], P(('mod', 'shard')), may hold values from -6 to 6
- labels_a: int32 [512, 1], P(('mod', 'shard')), may hold values from 0 to 3; in each aligned block of 16 rows (0 to 15, 16 to 31, ...) at most 6 rows name the same one
- grad_out_a: bfloat16 [512, 4096], P(('mod', 'shard')), may hold values from -6 to 6
- gate_saved: bfloat16 [4, 192, 11008], P('mod', None, 'shard'), may hold values from -6 to 6
- up_saved: bfloat16 [4, 192, 11008], P('mod', None, 'shard'), may hold values from -6 to 6
- gate_weight: bfloat16 [4, 4096, 11008], P('mod', None, 'shard'), may hold values from -0.09375 to 0.09375
- up_weight: bfloat16 [4, 4096, 11008], P('mod', None, 'shard'), may hold values from -0.09375 to 0.09375
- down_weight: bfloat16 [4, 11008, 4096], P('mod', 'shard'), may hold values from -0.0546875 to 0.0546875
Outputs:
- output_b: bfloat16 [512, 4096], P(('mod', 'shard'))
- grad_tokens_a: bfloat16 [512, 4096], P(('mod', 'shard'))
- grad_gate: bfloat16 [4, 4096, 11008], P('mod', None, 'shard')
- grad_up: bfloat16 [4, 4096, 11008], P('mod', None, 'shard')
- grad_down: bfloat16 [4, 11008, 4096], P('mod', 'shard')
Inputs may be any that keep to these rules, and one draw needn't show every extreme that they name: `labels_b`: among the 16 tokens of one home device no label occurs more than 6 times; in every draw some home device has exactly 6 tokens of one label. `labels_a`: among the 16 tokens of one home device no label occurs more than 6 times; in every draw some home device has exactly 6 tokens of one label.
All inputs are finite; a program needn't handle non-finite values.
Results may differ from a plain program's by a relative error of at most 0.0049.
Values may be sent and summed in bfloat16 or wider, within the bound.
A program may use at most 128 MiB of HBM per device.

v0:
```python
import jax
import jax.numpy as jnp
from jax import lax
from jax.sharding import PartitionSpec as P

CAP = 6


def place_table(labels, modes):
    lab = labels[:, 0]
    onehot = (lab[:, None] == jnp.arange(modes, dtype=jnp.int32)[None, :]).astype(jnp.int32)
    rank = jnp.cumsum(onehot, axis=0) - onehot
    slot = jnp.sum(rank * onehot, axis=1)
    within = (slot[:, None] == jnp.arange(CAP, dtype=jnp.int32)[None, :]).astype(jnp.int32)
    table = onehot[:, :, None] * within[:, None, :]
    return table.reshape(lab.shape[0], modes * CAP).astype(jnp.bfloat16)


def dispatch(place, values, modes):
    sent = lax.dot_general(
        place, values, (((0,), (0,)), ((), ())), preferred_element_type=jnp.float32
    )
    return sent.astype(jnp.bfloat16).reshape(modes, CAP, values.shape[1])


def collect(place, arrived):
    flat = arrived.reshape(place.shape[1], arrived.shape[2])
    return jnp.dot(place, flat, preferred_element_type=jnp.float32).astype(jnp.bfloat16)


def contract_last(left, right):
    return lax.dot_general(
        left, right, (((1,), (1,)), ((), ())), preferred_element_type=jnp.float32
    )


def forward_pass(tokens_b, labels_b, gate_w, up_w, down_w):
    modes = lax.axis_size("mod")
    width = tokens_b.shape[1]
    place = place_table(labels_b, modes)
    sent = dispatch(place, tokens_b, modes)
    arrived = lax.all_to_all(sent, "mod", split_axis=0, concat_axis=0, tiled=True)
    local_rows = arrived.reshape(modes * CAP, width)
    piece = lax.all_gather(local_rows, "shard", axis=0, tiled=True)
    gate = jnp.dot(piece, gate_w, preferred_element_type=jnp.float32)
    up = jnp.dot(piece, up_w, preferred_element_type=jnp.float32)
    terms = jnp.dot(
        (jax.nn.silu(gate) * up).astype(jnp.bfloat16), down_w, preferred_element_type=jnp.float32
    )
    summed = lax.psum_scatter(terms, "shard", scatter_dimension=0, tiled=True)
    back = summed.astype(jnp.bfloat16).reshape(modes, CAP, width)
    returned = lax.all_to_all(back, "mod", split_axis=0, concat_axis=0, tiled=True)
    return collect(place, returned)


def backward_pass(tokens_a, labels_a, grad_out_a, gate_s, up_s, gate_w, up_w, down_w):
    modes = lax.axis_size("mod")
    width = tokens_a.shape[1]
    place = place_table(labels_a, modes)
    sent_x = dispatch(place, tokens_a, modes)
    sent_g = dispatch(place, grad_out_a, modes)
    arrived_x, arrived_g = (
        lax.all_to_all(sent_x, "mod", split_axis=0, concat_axis=0, tiled=True),
        lax.all_to_all(sent_g, "mod", split_axis=0, concat_axis=0, tiled=True),
    )
    all_x, all_g = (
        lax.all_gather(arrived_x.reshape(modes * CAP, width), "shard", axis=0, tiled=True),
        lax.all_gather(arrived_g.reshape(modes * CAP, width), "shard", axis=0, tiled=True),
    )
    gate = gate_s.astype(jnp.float32)
    up = up_s.astype(jnp.float32)
    sig = jax.nn.sigmoid(gate)
    act = gate * sig
    dh = contract_last(all_g, down_w)
    dgate = (dh * up * sig * (1.0 + gate * (1.0 - sig))).astype(jnp.bfloat16)
    dup = (dh * act).astype(jnp.bfloat16)
    hidden = (act * up).astype(jnp.bfloat16)
    outer = (((0,), (0,)), ((), ()))
    grad_down = lax.dot_general(hidden, all_g, outer, preferred_element_type=jnp.float32).astype(
        jnp.bfloat16
    )
    grad_gate = lax.dot_general(all_x, dgate, outer, preferred_element_type=jnp.float32).astype(
        jnp.bfloat16
    )
    grad_up = lax.dot_general(all_x, dup, outer, preferred_element_type=jnp.float32).astype(
        jnp.bfloat16
    )
    terms = contract_last(dgate, gate_w) + contract_last(dup, up_w)
    summed = lax.psum_scatter(terms, "shard", scatter_dimension=0, tiled=True)
    back = summed.astype(jnp.bfloat16).reshape(modes, CAP, width)
    returned = lax.all_to_all(back, "mod", split_axis=0, concat_axis=0, tiled=True)
    return (collect(place, returned), grad_gate[None], grad_up[None], grad_down[None])


def body(
    tokens_b,
    labels_b,
    tokens_a,
    labels_a,
    grad_out_a,
    gate_saved,
    up_saved,
    gate_weight,
    up_weight,
    down_weight,
):
    gate_w = gate_weight[0]
    up_w = up_weight[0]
    down_w = down_weight[0]
    output_b = forward_pass(tokens_b, labels_b, gate_w, up_w, down_w)
    grads = backward_pass(
        tokens_a, labels_a, grad_out_a, gate_saved[0], up_saved[0], gate_w, up_w, down_w
    )
    return (output_b, grads[0], grads[1], grads[2], grads[3])


def solution(mesh):
    return jax.shard_map(
        body,
        mesh=mesh,
        in_specs=(
            P(("mod", "shard"), None),
            P(("mod", "shard"), None),
            P(("mod", "shard"), None),
            P(("mod", "shard"), None),
            P(("mod", "shard"), None),
            P("mod", None, "shard"),
            P("mod", None, "shard"),
            P("mod", None, "shard"),
            P("mod", None, "shard"),
            P("mod", "shard", None),
        ),
        out_specs=(
            P(("mod", "shard"), None),
            P(("mod", "shard"), None),
            P("mod", None, "shard"),
            P("mod", None, "shard"),
            P("mod", "shard", None),
        ),
        check_vma=False,
    )
```

profile of v0, /device:TPU:0, one launch (start us, length us, event | category | flops | bytes accessed | tf_op | source)
XLA Modules:
  0.0 327.6 jit_solution(9912826482816697624)
XLA Ops:
  7.2 0.0 copy-start
  7.2 0.0 copy-start.5
  7.2 0.0 copy-start.3
  7.2 0.0 all-gather.6.cloned.1.call-start
  7.2 0.8 fusion.44
  8.0 0.1 copy.18
  8.2 0.8 select_reduce_fusion
  9.0 0.0 copy-done
  9.0 0.2 convolution_convert_fusion.4
  9.2 0.1 reshape.137
  9.3 0.0 copy-start.4
  9.3 10.2 %all_to_all.25 = bf16[4,6,4096]{2,1,0:T(8,128)(2,1)S(1)} all-to-all(bf16[4,6,4096]{2,1,0:T(8,128)(2,1)S(1)} %reshape.137), channel_id=1, replica_groups=mesh['mod'=4,'shard'=8] {'mod'}, dimensions={0} | all-to-all | bytes 393216 | tf_op jit(solution)/shard_map/all_to_all | solution.py:64
  19.5 0.7 reshape.138
  20.3 0.0 all-gather.6.cloned.1.call-update
  20.3 0.0 all-gather.4.cloned.1.call-start
  20.3 0.0 copy-done.5
  20.3 0.1 fusion.45
  20.4 0.1 copy.17
  20.5 0.2 select_reduce_fusion.1
  20.7 0.0 copy-done.3
  20.8 0.2 convolution_convert_fusion.5
  20.9 0.1 reshape.134
  21.0 0.0 copy-start.8
  21.0 0.0 copy-start.9
  21.1 8.5 %all_to_all.26 = bf16[4,6,4096]{2,1,0:T(8,128)(2,1)S(1)} all-to-all(bf16[4,6,4096]{2,1,0:T(8,128)(2,1)S(1)} %reshape.134), channel_id=1, replica_groups=mesh['mod'=4,'shard'=8] {'mod'}, dimensions={0} | all-to-all | bytes 393216 | tf_op jit(solution)/shard_map/all_to_all | solution.py:42
  29.6 0.7 reshape.135
  30.3 0.0 all-gather.4.cloned.1.call-update
  30.4 0.0 all-gather.8.cloned.1.call-start
  30.4 0.2 convolution_convert_fusion.3
  30.6 0.1 reshape.140
  30.7 8.4 %all_to_all.27 = bf16[4,6,4096]{2,1,0:T(8,128)(2,1)S(1)} all-to-all(bf16[4,6,4096]{2,1,0:T(8,128)(2,1)S(1)} %reshape.140), channel_id=1, replica_groups=mesh['mod'=4,'shard'=8] {'mod'}, dimensions={0} | all-to-all | bytes 393216 | tf_op jit(solution)/shard_map/all_to_all | solution.py:63
  39.1 0.8 reshape.141
  39.8 0.0 all-gather.8.cloned.1.call-update
  39.9 0.0 reduce-scatter.5.cloned.1.call-start
  39.9 25.0 %all-gather.6.cloned.1.call-done = bf16[192,4096]{1,0:T(8,128)(2,1)} async-done(((bf16[24,4096]{1,0:T(8,128)(2,1)}), bf16[192,4096]{1,0:T(8,128)(2,1)}) %all-gather.6.cloned.1.call-update) | async-done | bytes 1572880 | tf_op jit(solution)/shard_map/all_gather | solution.py:68
  64.9 8.9 %fusion.30 = (bf16[192,1376]{1,0:T(8,128)(2,1)S(1)}, f32[192,1376]{1,0:T(8,128)S(1)}) fusion(bf16[1,192,1376]{2,1,0:T(8,128)(2,1)S(1)} %copy-done.8, bf16[1,192,1376]{2,1,0:T(8,128)(2,1)S(1)} %copy-done.9, bf16[192,4096]{1,0:T(8,128)(2,1)} %all-gather.6.cloned.1.call-done, bf16[1,1376,4096]{2,1,0:T(8,128)(2,1)} %param.19), kind=kOutput, calls=%fused_computation.35 | convolution fusion | flops 2167431168 | bytes 15486976 | tf_op jit(solution)/shard_map/dot_general | solution.py:32
  73.8 0.0 copy-start.10
  73.9 0.0 slice-start.2
  73.9 6.2 %fusion.7 = f32[192,4096]{1,0:T(8,128)S(1)} fusion(bf16[1,4096,1376]{1,2,0:T(8,128)(2,1)} %param.18, f32[192,1376]{1,0:T(8,128)S(1)} %get-tuple-element.6, bf16[1,192,1376]{2,1,0:T(8,128)(2,1)S(1)} %copy-done.9), kind=kOutput, calls=%fused_computation.10 | convolution fusion | flops 2166110208 | bytes 16003072 | tf_op jit(solution)/shard_map/dot_general | solution.py:32
  80.1 4.5 %fusion.15 = f32[192,4096]{1,0:T(8,128)} fusion(f32[192,4096]{1,0:T(8,128)S(1)} %fusion.7, bf16[192,1376]{1,0:T(8,128)(2,1)S(1)} %get-tuple-element.5, bf16[1,4096,1376]{1,2,0:T(8,128)(2,1)S(1)} %bitcast.80), kind=kOutput, calls=%fused_computation.18 | convolution fusion | flops 2165047296 | bytes 18092032 | tf_op jit(solution)/shard_map/dot_general | solution.py:32
  84.6 0.0 reduce-scatter.5.cloned.1.call-update
  84.6 0.2 reduce-scatter.3.cloned.1.call-start
  84.9 25.5 %all-gather.4.cloned.1.call-done = bf16[192,4096]{1,0:T(8,128)(2,1)} async-done(((bf16[24,4096]{1,0:T(8,128)(2,1)}), bf16[192,4096]{1,0:T(8,128)(2,1)}) %all-gather.4.cloned.1.call-update) | async-done | bytes 1572880 | tf_op jit(solution)/shard_map/all_gather | solution.py:44
  110.3 9.7 %fusion.13 = f32[192,1376]{1,0:T(8,128)} fusion(bf16[192,4096]{1,0:T(8,128)(2,1)} %all-gather.4.cloned.1.call-done, bf16[1,4096,1376]{1,2,0:T(8,128)(2,1)} %param.17), kind=kOutput, calls=%fused_computation.16 | convolution fusion | flops 2164260864 | bytes 13901824 | tf_op jit(solution)/shard_map/dot_general | solution.py:45
  120.0 15.8 %fusion.5 = f32[192,4096]{1,0:T(8,128)} fusion(bf16[1,1376,4096]{2,1,0:T(8,128)(2,1)} %param.19, bf16[192,4096]{1,0:T(8,128)(2,1)S(1)} %copy-done.7, bf16[1,4096,1376]{1,2,0:T(8,128)(2,1)} %param.18, f32[192,1376]{1,0:T(8,128)} %fusion.13), kind=kOutput, calls=%fused_computation.8 | convolution fusion | flops 4330106880 | bytes 28319744 | tf_op jit(solution)/shard_map/dot_general | solution.py:47
  135.9 0.0 reduce-scatter.3.cloned.1.call-update
  135.9 1.5 copy-done.6
  137.4 7.1 %fusion = bf16[1,1376,4096]{2,1,0:T(8,128)(2,1)} fusion(bf16[192,4096]{1,0:T(8,128)(2,1)S(1)} %copy-done.6, bf16[1,192,1376]{2,1,0:T(8,128)(2,1)S(1)} %copy-done.8, bf16[1,192,1376]{2,1,0:T(8,128)(2,1)} %param.15), kind=kOutput, calls=%fused_computation.3 | convolution fusion | flops 2172010496 | bytes 13901824 | tf_op jit(solution)/shard_map/dot_general | solution.py:79
  144.6 10.6 %all-gather.8.cloned.1.call-done = bf16[192,4096]{1,0:T(8,128)(2,1)} async-done(((bf16[24,4096]{1,0:T(8,128)(2,1)}), bf16[192,4096]{1,0:T(8,128)(2,1)}) %all-gather.8.cloned.1.call-update) | async-done | bytes 1572880 | tf_op jit(solution)/shard_map/all_gather | solution.py:67
  155.1 9.5 %fusion.2 = bf16[1,4096,1376]{1,2,0:T(8,128)(2,1)} fusion(bf16[192,4096]{1,0:T(8,128)(2,1)} %all-gather.8.cloned.1.call-done, f32[192,1376]{1,0:T(8,128)} %copy-done.10, bf16[1,192,1376]{2,1,0:T(8,128)(2,1)} %param.15), kind=kOutput, calls=%fused_computation.5 | convolution fusion | flops 2171746304 | bytes 14430208 | tf_op jit(solution)/shard_map/dot_general | solution.py:85
  164.6 67.3 %reduce-scatter.5.cloned.1.call-done = f32[24,4096]{1,0:T(8,128)} async-done(((f32[192,4096]{1,0:T(8,128)}), f32[24,4096]{1,0:T(8,128)}) %reduce-scatter.5.cloned.1.call-update) | async-done | bytes 393232 | tf_op jit(solution)/shard_map/reduce_scatter | solution.py:89
  231.9 1.0 convert_element_type.115
  232.9 0.8 reshape.139
  233.7 3.4 %all-to-all-start.3 = ((bf16[4,6,4096]{2,1,0:T(8,128)(2,1)}), bf16[4,6,4096]{2,1,0:T(8,128)(2,1)S(1)}, u32[]{:S(2)}, u32[]{:S(2)}) async-start(bf16[4,6,4096]{2,1,0:T(8,128)(2,1)} %reshape.139), calls=%async_computation.5 | async-start | bytes 524288 | tf_op jit(solution)/shard_map/all_to_all | solution.py:91
  237.1 0.0 copy-start.1
  237.1 6.0 %fusion.1 = bf16[1,4096,1376]{1,2,0:T(8,128)(2,1)} fusion(bf16[192,4096]{1,0:T(8,128)(2,1)S(1)} %copy-done.2, bf16[192,1376]{1,0:T(8,128)(2,1)S(1)} %get-tuple-element.5), kind=kOutput, calls=%fused_computation.4 | convolution fusion | flops 2169896960 | bytes 13373440 | tf_op jit(solution)/shard_map/dot_general | solution.py:82
  243.2 65.8 %reduce-scatter.3.cloned.1.call-done = f32[24,4096]{1,0:T(8,128)} async-done(((f32[192,4096]{1,0:T(8,128)}), f32[24,4096]{1,0:T(8,128)}) %reduce-scatter.3.cloned.1.call-update) | async-done | bytes 393232 | tf_op jit(solution)/shard_map/reduce_scatter | solution.py:50
  309.0 1.0 convert_element_type.102
  310.0 0.8 reshape.136
  310.8 0.0 all-to-all-done.3
  310.8 3.4 %all-to-all-start.1 = ((bf16[4,6,4096]{2,1,0:T(8,128)(2,1)}), bf16[4,6,4096]{2,1,0:T(8,128)(2,1)S(1)}, u32[]{:S(2)}, u32[]{:S(2)}) async-start(bf16[4,6,4096]{2,1,0:T(8,128)(2,1)} %reshape.136), calls=%async_computation.2 | async-start | bytes 524288 | tf_op jit(solution)/shard_map/all_to_all | solution.py:52
  314.2 0.9 fusion.19
  315.1 5.1 %all-to-all-done.1 = bf16[4,6,4096]{2,1,0:T(8,128)(2,1)S(1)} async-done(((bf16[4,6,4096]{2,1,0:T(8,128)(2,1)}), bf16[4,6,4096]{2,1,0:T(8,128)(2,1)S(1)}, u32[]{:S(2)}, u32[]{:S(2)}) %all-to-all-start.1) | async-done | bytes 196640 | tf_op jit(solution)/shard_map/all_to_all | solution.py:52
  320.2 0.9 fusion.18
  (24 shorter events, 0.2 us)
Async XLA Ops:
  7.2 1.9 copy-start
  7.2 13.1 %copy-start.5 = (s32[16,1]{0,1:T(1,128)S(1)}, s32[16,1]{0,1:T(1,128)}, u32[]{:S(2)}) copy-start(s32[16,1]{0,1:T(1,128)} %param.11) | copy-start | bytes 196
  7.2 13.6 %copy-start.3 = (bf16[16,4096]{1,0:T(8,128)(2,1)S(1)}, bf16[16,4096]{1,0:T(8,128)(2,1)}, u32[]{:S(2)}) copy-start(bf16[16,4096]{1,0:T(8,128)(2,1)} %param.10) | copy-start | bytes 393220
  7.2 57.7 %all-gather.6.cloned.1.call-start = ((), (), s32[]{:S(2)}) async-start(), calls=%async_computation.9 | async-start | bytes 1769472 | tf_op jit(solution)/shard_map/all_gather | solution.py:68
  9.3 21.1 %copy-start.4 = (bf16[16,4096]{1,0:T(8,128)(2,1)S(1)}, bf16[16,4096]{1,0:T(8,128)(2,1)}, u32[]{:S(2)}) copy-start(bf16[16,4096]{1,0:T(8,128)(2,1)} %param.12) | copy-start | bytes 393220
  20.3 90.0 %all-gather.4.cloned.1.call-start = ((), (), s32[]{:S(2)}) async-start(), calls=%async_computation.7 | async-start | bytes 1769472 | tf_op jit(solution)/shard_map/all_gather | solution.py:44
  21.0 43.9 %copy-start.8 = (bf16[1,192,1376]{2,1,0:T(8,128)(2,1)S(1)}, bf16[1,192,1376]{2,1,0:T(8,128)(2,1)}, u32[]{:S(2)}) copy-start(bf16[1,192,1376]{2,1,0:T(8,128)(2,1)} %param.16) | copy-start | bytes 1585156
  21.0 43.9 %copy-start.9 = (bf16[1,192,1376]{2,1,0:T(8,128)(2,1)S(1)}, bf16[1,192,1376]{2,1,0:T(8,128)(2,1)}, u32[]{:S(2)}) copy-start(bf16[1,192,1376]{2,1,0:T(8,128)(2,1)} %param.15) | copy-start | bytes 1585156
  30.4 124.8 %all-gather.8.cloned.1.call-start = ((), (), s32[]{:S(2)}) async-start(), calls=%async_computation.11 | async-start | bytes 1769472 | tf_op jit(solution)/shard_map/all_gather | solution.py:67
  39.9 192.0 %reduce-scatter.5.cloned.1.call-start = ((), (), s32[]{:S(2)}) async-start(), calls=%async_computation.10 | async-start | bytes 3538944 | tf_op jit(solution)/shard_map/reduce_scatter | solution.py:89
  64.9 15.2 %slice-start = ((s8[11272192]{0:T(1024)(128)(4,1)}), s8[4194304]{0:T(1024)(128)(4,1)S(1)}, s32[]{:S(2)}) async-start(s8[11272192]{0:T(1024)(128)(4,1)} %bitcast.79), calls=%async_computation.12 | async-start | bytes 8388608
  64.9 15.2 %slice-start.1 = ((s8[11272192]{0:T(1024)(128)(4,1)}), s8[2883584]{0:T(1024)(128)(4,1)S(1)}, s32[]{:S(2)}) async-start(s8[11272192]{0:T(1024)(128)(4,1)} %bitcast.79), calls=%async_computation.13 | async-start | bytes 5767168
  73.8 6.3 %copy-start.10 = (f32[192,1376]{1,0:T(8,128)}, f32[192,1376]{1,0:T(8,128)S(1)}, u32[]{:S(2)}) copy-start(f32[192,1376]{1,0:T(8,128)S(1)} %get-tuple-element.6) | copy-start | bytes 3170308
  73.9 6.3 %slice-start.2 = ((s8[11272192]{0:T(1024)(128)(4,1)}), s8[4194304]{0:T(1024)(128)(4,1)S(1)}, s32[]{:S(2)}) async-start(s8[11272192]{0:T(1024)(128)(4,1)} %bitcast.79), calls=%async_computation.14 | async-start | bytes 8388608
  84.6 224.4 %reduce-scatter.3.cloned.1.call-start = ((), (), s32[]{:S(2)}) async-start(), calls=%async_computation.8 | async-start | bytes 3538944 | tf_op jit(solution)/shard_map/reduce_scatter | solution.py:50
  110.3 9.7 %copy-start.7 = (bf16[192,4096]{1,0:T(8,128)(2,1)S(1)}, bf16[192,4096]{1,0:T(8,128)(2,1)}, u32[]{:S(2)}) copy-start(bf16[192,4096]{1,0:T(8,128)(2,1)} %all-gather.4.cloned.1.call-done) | copy-start | bytes 4718596
  135.9 1.6 copy-start.6
  155.1 82.0 %copy-start.2 = (bf16[192,4096]{1,0:T(8,128)(2,1)S(1)}, bf16[192,4096]{1,0:T(8,128)(2,1)}, u32[]{:S(2)}) copy-start(bf16[192,4096]{1,0:T(8,128)(2,1)} %all-gather.8.cloned.1.call-done) | copy-start | bytes 4718596
  233.7 77.1 %all-to-all-start.3 = ((bf16[4,6,4096]{2,1,0:T(8,128)(2,1)}), bf16[4,6,4096]{2,1,0:T(8,128)(2,1)S(1)}, u32[]{:S(2)}, u32[]{:S(2)}) async-start(bf16[4,6,4096]{2,1,0:T(8,128)(2,1)} %reshape.139), calls=%async_computation.5 | async-start | bytes 524288 | tf_op jit(solution)/shard_map/all_to_all | solution.py:91
  237.1 83.9 %copy-start.1 = (bf16[16,4096]{1,0:T(8,128)(2,1)S(1)}, bf16[16,4096]{1,0:T(8,128)(2,1)}, u32[]{:S(2)}) copy-start(bf16[16,4096]{1,0:T(8,128)(2,1)} %param.14) | copy-start | bytes 393220
  310.8 9.4 %all-to-all-start.1 = ((bf16[4,6,4096]{2,1,0:T(8,128)(2,1)}), bf16[4,6,4096]{2,1,0:T(8,128)(2,1)S(1)}, u32[]{:S(2)}, u32[]{:S(2)}) async-start(bf16[4,6,4096]{2,1,0:T(8,128)(2,1)} %reshape.136), calls=%async_computation.2 | async-start | bytes 524288 | tf_op jit(solution)/shard_map/all_to_all | solution.py:52
Sparse Core Ops, SparseCore 0:
  20.4 44.4 all-gather.5
  67.7 42.5 all-gather.3
  112.5 42.5 all-gather.7
  159.1 72.7 reduce-scatter.4
  235.3 73.6 reduce-scatter.2
where the time goes:
time: 328 us
  waiting for transfers between devices  199 us (61%)
  matrix products  70.1 us (21%)
  blocking collectives  27.1 us (8%)
  between operations  14 us (4%)
  starting transfers between devices  7.2 us (2%)
  local copies, waits for them, and re-layouts  5.84 us (2%)
  other arithmetic  4.02 us (1%)
    reduce_scatter x1, waiting for transfers between devices, backward_pass(): summed = lax.psum_scatter(terms, 'shard', scatter_dimension=0, tiled=True)  67.3 us
    reduce_scatter x1, waiting for transfers between devices, forward_pass(): summed = lax.psum_scatter(terms, 'shard', scatter_dimension=0, tiled=True)  65.8 us
    all_gather x1, waiting for transfers between devices, forward_pass(): piece = lax.all_gather(local_rows, 'shard', axis=0, tiled=True)  25.5 us
    all_gather x1, waiting for transfers between devices, backward_pass(): lax.all_gather(arrived_g.reshape(modes * CAP, width), 'shard', axis=0, ti...  25 us
    dot_general x3, matrix products, contract_last(): lax.dot_general(left, right, (((1,), (1,)), ((), ())), preferred_element_...  19.6 us
    dot_general x1, matrix products, forward_pass(): jnp.dot((jax.nn.silu(gate) * up).astype(jnp.bfloat16), down_w, preferred_...  15.8 us
    all_gather x1, waiting for transfers between devices, backward_pass(): lax.all_gather(arrived_x.reshape(modes * CAP, width), 'shard', axis=0, ti...  10.6 us
    all_to_all x1, blocking collectives, backward_pass(): lax.all_to_all(sent_g, 'mod', split_axis=0, concat_axis=0, tiled=True)  10.2 us
  transfers between devices with their start and end apart: 7, of which 6 were waited for; matrix products, arithmetic and copies ran while one was open for 23% of the time, Pallas kernels for 0%

commit v1 on v0

--- a/solution.py
+++ b/solution.py
@@ -4,6 +4,18 @@
 from jax.sharding import PartitionSpec as P
 
 CAP = 6
+
+
+def collect_2(value, axis, dim):
+    ways, here, step = (lax.axis_size(axis), lax.axis_index(axis), value.shape[dim])
+    line, have = (value, 1)
+    while have < ways:
+        line = jnp.concatenate(
+            [line, lax.ppermute(line, axis, [(d, (d - have) % ways) for d in range(ways)])],
+            axis=dim,
+        )
+        have = 2 * have
+    return jnp.roll(line, here * step, axis=dim)
 
 
 def place_table(labels, modes):
@@ -41,7 +53,7 @@
     sent = dispatch(place, tokens_b, modes)
     arrived = lax.all_to_all(sent, "mod", split_axis=0, concat_axis=0, tiled=True)
     local_rows = arrived.reshape(modes * CAP, width)
-    piece = lax.all_gather(local_rows, "shard", axis=0, tiled=True)
+    piece = collect_2(local_rows, "shard", 0)
     gate = jnp.dot(piece, gate_w, preferred_element_type=jnp.float32)
     up = jnp.dot(piece, up_w, preferred_element_type=jnp.float32)
     terms = jnp.dot(

time: 328 us -> 308 us (0.939)
  waiting for transfers between devices: 199 us -> 177 us
  blocking collectives: 27.1 us -> 18.6 us
  starting transfers between devices: 7.2 us -> 15.7 us
    ppermute x0 -> x3, waiting for transfers between devices: none -> 55.5 us  [collect_2(): lax.ppermute(line, axis, [(d, (d - have) % ways) for d in range(ways)])]
    all_gather x1 -> x0, waiting for transfers between devices: 25.5 us -> none  [forward_pass(): piece = lax.all_gather(local_rows, 'shard', axis=0, tiled=True)]
    all_gather x1, waiting for transfers between devices: 25 us -> 0.02 us  [backward_pass(): lax.all_gather(arrived_g.reshape(modes * CAP, width), 'shard', axis=0, ti...]
    reduce_scatter x1, waiting for transfers between devices: 65.8 us -> 44.7 us  [forward_pass(): summed = lax.psum_scatter(terms, 'shard', scatter_dimension=0, tiled=True)]
    all_gather x1, waiting for transfers between devices: 10.6 us -> 0.01 us  [backward_pass(): lax.all_gather(arrived_x.reshape(modes * CAP, width), 'shard', axis=0, ti...]
    all_to_all x1 -> x0, blocking collectives: 8.39 us -> none  [backward_pass(): lax.all_to_all(sent_x, 'mod', split_axis=0, concat_axis=0, tiled=True)]
    all_to_all x0 -> x1, waiting for transfers between devices: none -> 5.9 us  [backward_pass(): lax.all_to_all(sent_x, 'mod', split_axis=0, concat_axis=0, tiled=True)]
    ppermute x0 -> x3, starting transfers between devices: none -> 5.18 us  [collect_2(): lax.ppermute(line, axis, [(d, (d - have) % ways) for d in range(ways)])]
  transfers between devices with their start and end apart: 7 -> 10, of which waited for: 6 -> 6; matrix products, arithmetic and copies ran while one was open for 23% -> 24% of each run, Pallas kernels for 0% -> 0%
where the time goes in v1:
time: 308 us; the launch traced here: 307 us
  waiting for transfers between devices  177 us (57%)
  matrix products  68.9 us (22%)
  blocking collectives  18.6 us (6%)
  starting transfers between devices  15.7 us (5%)
  between operations  14.1 us (5%)
  local copies, waits for them, and re-layouts  8.52 us (3%)
  other arithmetic  4.1 us (1%)
    reduce_scatter x1, waiting for transfers between devices, backward_pass(): summed = lax.psum_scatter(terms, 'shard', scatter_dimension=0, tiled=True)  65.7 us
    ppermute x3, waiting for transfers between devices, collect_2(): lax.ppermute(line, axis, [(d, (d - have) % ways) for d in range(ways)])  55.5 us
    reduce_scatter x1, waiting for transfers between devices, forward_pass(): summed = lax.psum_scatter(terms, 'shard', scatter_dimension=0, tiled=True)  44.7 us
    dot_general x3, matrix products, contract_last(): lax.dot_general(left, right, (((1,), (1,)), ((), ())), preferred_element_...  19.5 us
    dot_general x1, matrix products, forward_pass(): jnp.dot((jax.nn.silu(gate) * up).astype(jnp.bfloat16), down_w, preferred_...  16.1 us
    all_to_all x1, blocking collectives, backward_pass(): lax.all_to_all(sent_g, 'mod', split_axis=0, concat_axis=0, tiled=True)  10.2 us
    dot_general x1, matrix products, backward_pass(): lax.dot_general(all_x, dup, outer, preferred_element_type=jnp.float32)  9.5 us
    all_to_all x1, blocking collectives, forward_pass(): lax.all_to_all(sent, 'mod', split_axis=0, concat_axis=0, tiled=True)  8.39 us
  transfers between devices with their start and end apart: 10, of which 6 were waited for; matrix products, arithmetic and copies ran while one was open for 24% of the time, Pallas kernels for 0%

profile of v1, /device:TPU:0, one launch (start us, length us, event | category | flops | bytes accessed | tf_op | source)
XLA Modules:
  0.0 306.8 jit_solution(11145825640326335400)
XLA Ops:
  7.2 0.0 copy-start
  7.2 0.0 all-gather.3.cloned.1.call-start
  7.2 0.8 fusion.41
  8.0 0.1 copy.18
  8.2 0.8 select_reduce_fusion
  9.0 0.2 convolution_convert_fusion.4
  9.2 0.1 reshape.137
  9.3 0.0 copy-start.4
  9.3 10.2 %all_to_all.25 = bf16[4,6,4096]{2,1,0:T(8,128)(2,1)S(1)} all-to-all(bf16[4,6,4096]{2,1,0:T(8,128)(2,1)S(1)} %reshape.137), channel_id=1, replica_groups=mesh['mod'=4,'shard'=8] {'mod'}, dimensions={0} | all-to-all | bytes 393216 | tf_op jit(solution)/shard_map/all_to_all | solution.py:76
  19.5 0.7 reshape.138
  20.3 0.0 all-gather.3.cloned.1.call-update
  20.3 0.1 fusion.42
  20.4 0.1 copy.17
  20.5 0.2 select_reduce_fusion.1
  20.7 0.2 convolution_convert_fusion.5
  20.9 0.1 reshape.134
  21.0 8.4 %all_to_all.26 = bf16[4,6,4096]{2,1,0:T(8,128)(2,1)S(1)} all-to-all(bf16[4,6,4096]{2,1,0:T(8,128)(2,1)S(1)} %reshape.134), channel_id=1, replica_groups=mesh['mod'=4,'shard'=8] {'mod'}, dimensions={0} | all-to-all | bytes 393216 | tf_op jit(solution)/shard_map/all_to_all | solution.py:54
  29.4 0.1 reshape.135
  29.4 4.6 %collective-permute-start = (bf16[24,4096]{1,0:T(8,128)(2,1)S(1)}, bf16[24,4096]{1,0:T(8,128)(2,1)S(1)}, u32[]{:S(2)}, u32[]{:S(2)}) collective-permute-start(bf16[24,4096]{1,0:T(8,128)(2,1)S(1)} %reshape.135), channel_id=1, source_target_pairs={{0,7},{1,0},{2,1},{3,2},{4,3},{5,4},{6,5},{7,6},{8,15},{9,8},{10,9... | collective-permute-start | bytes 589832 | tf_op jit(solution)/shard_map/ppermute | solution.py:14
  34.1 0.2 convolution_convert_fusion.3
  34.3 0.8 reshape.140
  35.0 3.4 %all-to-all-start.4 = ((bf16[4,6,4096]{2,1,0:T(8,128)(2,1)}), bf16[4,6,4096]{2,1,0:T(8,128)(2,1)S(1)}, u32[]{:S(2)}, u32[]{:S(2)}) async-start(bf16[4,6,4096]{2,1,0:T(8,128)(2,1)} %reshape.140), calls=%async_computation.6 | async-start | bytes 524288 | tf_op jit(solution)/shard_map/all_to_all | solution.py:75
  38.4 0.0 all-gather.5.cloned.1.call-start
  38.5 5.9 %all-to-all-done.4 = bf16[4,6,4096]{2,1,0:T(8,128)(2,1)S(1)} async-done(((bf16[4,6,4096]{2,1,0:T(8,128)(2,1)}), bf16[4,6,4096]{2,1,0:T(8,128)(2,1)S(1)}, u32[]{:S(2)}, u32[]{:S(2)}) %all-to-all-start.4) | async-done | bytes 196640 | tf_op jit(solution)/shard_map/all_to_all | solution.py:75
  44.4 0.8 reshape.141
  45.2 0.0 all-gather.5.cloned.1.call-update
  45.2 0.0 reduce-scatter.3.cloned.1.call-start
  45.3 0.5 collective-permute-start.1
  45.8 22.7 %collective-permute-done.1 = bf16[48,4096]{1,0:T(8,128)(2,1)S(1)} collective-permute-done((bf16[48,4096]{1,0:T(8,128)(2,1)S(1)}, bf16[48,4096]{1,0:T(8,128)(2,1)S(1)}, u32[]{:S(2)}, u32[]{:S(2)}) %collective-permute-start.1) | collective-permute-done | bytes 393248 | tf_op jit(solution)/shard_map/ppermute | solution.py:14
  68.5 0.1 pad_maximum_fusion
  68.6 0.1 collective-permute-start.2
  68.7 32.7 %collective-permute-done.2 = bf16[96,4096]{1,0:T(8,128)(2,1)S(1)} collective-permute-done((bf16[96,4096]{1,0:T(8,128)(2,1)S(1)}, bf16[96,4096]{1,0:T(8,128)(2,1)S(1)}, u32[]{:S(2)}, u32[]{:S(2)}) %collective-permute-start.2) | collective-permute-done | bytes 786464 | tf_op jit(solution)/shard_map/ppermute | solution.py:14
  101.5 0.1 constant_dynamic-update-slice_fusion.4
  101.6 0.1 constant_dynamic-update-slice_fusion
  101.7 0.0 copy-start.5
  101.7 1.7 copy-done.5
  103.3 8.2 %fusion.9 = f32[192,1376]{1,0:T(8,128)S(1)} fusion(bf16[1,4096,1376]{1,2,0:T(8,128)(2,1)} %param.18, bf16[384,4096]{1,0:T(8,128)(2,1)S(1)} %constant_dynamic-update-slice_fusion, s32[]{:T(128)S(6)} %select_n.14), kind=kOutput, calls=%fused_computation.12 | convolution fusion | flops 2164260864 | bytes 13901828 | tf_op jit(solution)/shard_map/dot_general | solution.py:58
  111.6 16.1 %fusion.5 = f32[192,4096]{1,0:T(8,128)} fusion(bf16[1,1376,4096]{2,1,0:T(8,128)(2,1)} %param.19, f32[192,1376]{1,0:T(8,128)S(1)} %fusion.9, bf16[1,4096,1376]{1,2,0:T(8,128)(2,1)} %param.17, bf16[384,4096]{1,0:T(8,128)(2,1)} %copy-done.5, s32[]{:T(128)S(6)} %select_n.14), kind=kOutput, calls=%fused_computation.8 | convolution fusion | flops 4330106880 | bytes 28319748 | tf_op jit(solution)/shard_map/dot_general | solution.py:59
  127.7 0.0 reduce-scatter.3.cloned.1.call-update
  127.7 0.2 reduce-scatter.5.cloned.1.call-start
  128.0 0.0 all-gather.3.cloned.1.call-done
  128.0 0.8 copy-done.8
  128.8 0.2 copy-done.9
  128.9 8.9 %fusion.24 = (bf16[192,1376]{1,0:T(8,128)(2,1)S(1)}, f32[192,1376]{1,0:T(8,128)S(1)}) fusion(bf16[1,192,1376]{2,1,0:T(8,128)(2,1)S(1)} %copy-done.8, bf16[1,192,1376]{2,1,0:T(8,128)(2,1)S(1)} %copy-done.9, bf16[192,4096]{1,0:T(8,128)(2,1)} %all-gather.3.cloned.1.call-done, bf16[1,1376,4096]{2,1,0:T(8,128)(2,1)} %param.19), kind=kOutput, calls=%fused_computation.35 | convolution fusion | flops 2167431168 | bytes 15486976 | tf_op jit(solution)/shard_map/dot_general | solution.py:44
  137.8 0.0 slice-start.2
  137.9 6.2 %fusion.7 = f32[192,4096]{1,0:T(8,128)S(1)} fusion(bf16[1,4096,1376]{1,2,0:T(8,128)(2,1)} %param.18, f32[192,1376]{1,0:T(8,128)S(1)} %get-tuple-element.6, bf16[1,192,1376]{2,1,0:T(8,128)(2,1)S(1)} %copy-done.9), kind=kOutput, calls=%fused_computation.10 | convolution fusion | flops 2166110208 | bytes 16003072 | tf_op jit(solution)/shard_map/dot_general | solution.py:44
  144.1 4.4 %fusion.15 = f32[192,4096]{1,0:T(8,128)} fusion(f32[192,4096]{1,0:T(8,128)S(1)} %fusion.7, bf16[192,1376]{1,0:T(8,128)(2,1)S(1)} %get-tuple-element.5, bf16[1,4096,1376]{1,2,0:T(8,128)(2,1)S(1)} %bitcast.76), kind=kOutput, calls=%fused_computation.18 | convolution fusion | flops 2165047296 | bytes 18092032 | tf_op jit(solution)/shard_map/dot_general | solution.py:44
  148.5 0.0 reduce-scatter.5.cloned.1.call-update
  148.6 1.4 copy-done.7
  149.9 7.1 %fusion = bf16[1,1376,4096]{2,1,0:T(8,128)(2,1)} fusion(bf16[192,4096]{1,0:T(8,128)(2,1)S(1)} %copy-done.7, bf16[1,192,1376]{2,1,0:T(8,128)(2,1)S(1)} %copy-done.8, bf16[1,192,1376]{2,1,0:T(8,128)(2,1)} %param.15), kind=kOutput, calls=%fused_computation.3 | convolution fusion | flops 2172010496 | bytes 13901824 | tf_op jit(solution)/shard_map/dot_general | solution.py:91
  157.1 9.5 %fusion.2 = bf16[1,4096,1376]{1,2,0:T(8,128)(2,1)} fusion(bf16[192,4096]{1,0:T(8,128)(2,1)} %all-gather.5.cloned.1.call-done, f32[192,1376]{1,0:T(8,128)} %copy-done.10, bf16[1,192,1376]{2,1,0:T(8,128)(2,1)} %param.15), kind=kOutput, calls=%fused_computation.5 | convolution fusion | flops 2171746304 | bytes 14430208 | tf_op jit(solution)/shard_map/dot_general | solution.py:97
  166.6 44.7 %reduce-scatter.3.cloned.1.call-done = f32[24,4096]{1,0:T(8,128)} async-done(((f32[192,4096]{1,0:T(8,128)}), f32[24,4096]{1,0:T(8,128)}) %reduce-scatter.3.cloned.1.call-update) | async-done | bytes 393232 | tf_op jit(solution)/shard_map/reduce_scatter | solution.py:62
  211.3 1.0 convert_element_type.102
  212.3 0.8 reshape.136
  213.1 3.4 %all-to-all-start.1 = ((bf16[4,6,4096]{2,1,0:T(8,128)(2,1)}), bf16[4,6,4096]{2,1,0:T(8,128)(2,1)S(1)}, u32[]{:S(2)}, u32[]{:S(2)}) async-start(bf16[4,6,4096]{2,1,0:T(8,128)(2,1)} %reshape.136), calls=%async_computation.2 | async-start | bytes 524288 | tf_op jit(solution)/shard_map/all_to_all | solution.py:64
  216.5 0.0 copy-start.1
  216.5 6.0 %fusion.1 = bf16[1,4096,1376]{1,2,0:T(8,128)(2,1)} fusion(bf16[192,4096]{1,0:T(8,128)(2,1)S(1)} %copy-done.2, bf16[192,1376]{1,0:T(8,128)(2,1)S(1)} %get-tuple-element.5), kind=kOutput, calls=%fused_computation.4 | convolution fusion | flops 2169896960 | bytes 13373440 | tf_op jit(solution)/shard_map/dot_general | solution.py:94
  222.5 65.7 %reduce-scatter.5.cloned.1.call-done = f32[24,4096]{1,0:T(8,128)} async-done(((f32[192,4096]{1,0:T(8,128)}), f32[24,4096]{1,0:T(8,128)}) %reduce-scatter.5.cloned.1.call-update) | async-done | bytes 393232 | tf_op jit(solution)/shard_map/reduce_scatter | solution.py:101
  288.2 1.0 convert_element_type.115
  289.3 0.8 reshape.139
  290.0 3.4 %all-to-all-start.3 = ((bf16[4,6,4096]{2,1,0:T(8,128)(2,1)}), bf16[4,6,4096]{2,1,0:T(8,128)(2,1)S(1)}, u32[]{:S(2)}, u32[]{:S(2)}) async-start(bf16[4,6,4096]{2,1,0:T(8,128)(2,1)} %reshape.139), calls=%async_computation.5 | async-start | bytes 524288 | tf_op jit(solution)/shard_map/all_to_all | solution.py:103
  293.4 0.9 fusion.18
  294.3 5.1 %all-to-all-done.3 = bf16[4,6,4096]{2,1,0:T(8,128)(2,1)S(1)} async-done(((bf16[4,6,4096]{2,1,0:T(8,128)(2,1)}), bf16[4,6,4096]{2,1,0:T(8,128)(2,1)S(1)}, u32[]{:S(2)}, u32[]{:S(2)}) %all-to-all-start.3) | async-done | bytes 196640 | tf_op jit(solution)/shard_map/all_to_all | solution.py:103
  299.4 0.9 fusion.19
  (38 shorter events, 0.3 us)
Async XLA Ops:
  7.2 1.9 copy-start
  7.2 13.1 %copy-start.6 = (s32[16,1]{0,1:T(1,128)S(1)}, s32[16,1]{0,1:T(1,128)}, u32[]{:S(2)}) copy-start(s32[16,1]{0,1:T(1,128)} %param.11) | copy-start | bytes 196
  7.2 13.5 %copy-start.3 = (bf16[16,4096]{1,0:T(8,128)(2,1)S(1)}, bf16[16,4096]{1,0:T(8,128)(2,1)}, u32[]{:S(2)}) copy-start(bf16[16,4096]{1,0:T(8,128)(2,1)} %param.10) | copy-start | bytes 393220
  7.2 120.8 %all-gather.3.cloned.1.call-start = ((), (), s32[]{:S(2)}) async-start(), calls=%async_computation.8 | async-start | bytes 1769472 | tf_op jit(solution)/shard_map/all_gather | solution.py:80
  9.3 24.7 %copy-start.4 = (bf16[16,4096]{1,0:T(8,128)(2,1)S(1)}, bf16[16,4096]{1,0:T(8,128)(2,1)}, u32[]{:S(2)}) copy-start(bf16[16,4096]{1,0:T(8,128)(2,1)} %param.12) | copy-start | bytes 393220
  29.4 15.8 %collective-permute-start = (bf16[24,4096]{1,0:T(8,128)(2,1)S(1)}, bf16[24,4096]{1,0:T(8,128)(2,1)S(1)}, u32[]{:S(2)}, u32[]{:S(2)}) collective-permute-start(bf16[24,4096]{1,0:T(8,128)(2,1)S(1)} %reshape.135), channel_id=1, source_target_pairs={{0,7},{1,0},{2,1},{3,2},{4,3},{5,4},{6,5},{7,6},{8,15},{9,8},{10,9... | collective-permute-start | bytes 589832 | tf_op jit(solution)/shard_map/ppermute | solution.py:14
  35.0 9.4 %all-to-all-start.4 = ((bf16[4,6,4096]{2,1,0:T(8,128)(2,1)}), bf16[4,6,4096]{2,1,0:T(8,128)(2,1)S(1)}, u32[]{:S(2)}, u32[]{:S(2)}) async-start(bf16[4,6,4096]{2,1,0:T(8,128)(2,1)} %reshape.140), calls=%async_computation.6 | async-start | bytes 524288 | tf_op jit(solution)/shard_map/all_to_all | solution.py:75
  38.4 118.6 %all-gather.5.cloned.1.call-start = ((), (), s32[]{:S(2)}) async-start(), calls=%async_computation.10 | async-start | bytes 1769472 | tf_op jit(solution)/shard_map/all_gather | solution.py:79
  45.2 166.1 %reduce-scatter.3.cloned.1.call-start = ((), (), s32[]{:S(2)}) async-start(), calls=%async_computation.7 | async-start | bytes 3538944 | tf_op jit(solution)/shard_map/reduce_scatter | solution.py:62
  45.3 23.2 %collective-permute-start.1 = (bf16[48,4096]{1,0:T(8,128)(2,1)S(1)}, bf16[48,4096]{1,0:T(8,128)(2,1)S(1)}, u32[]{:S(2)}, u32[]{:S(2)}) collective-permute-start(bf16[48,4096]{1,0:T(8,128)(2,1)S(1)} %pad_maximum_fusion.1), channel_id=1, source_target_pairs={{0,6},{1,7},{2,0},{3,1},{4,2},{5,3},{6,4},{7,5},{8,14},{9,15},{10,... | collective-permute-start | bytes 1179656 | tf_op jit(solution)/shard_map/ppermute | solution.py:14
  68.6 32.9 %collective-permute-start.2 = (bf16[96,4096]{1,0:T(8,128)(2,1)S(1)}, bf16[96,4096]{1,0:T(8,128)(2,1)S(1)}, u32[]{:S(2)}, u32[]{:S(2)}) collective-permute-start(bf16[96,4096]{1,0:T(8,128)(2,1)S(1)} %pad_maximum_fusion), channel_id=1, source_target_pairs={{0,4},{1,5},{2,6},{3,7},{4,0},{5,1},{6,2},{7,3},{8,12},{9,13},{10,... | collective-permute-start | bytes 2359304 | tf_op jit(solution)/shard_map/ppermute | solution.py:14
  101.7 1.7 copy-start.5
  127.7 1.1 copy-start.8
  127.7 1.2 copy-start.9
  127.7 160.5 %reduce-scatter.5.cloned.1.call-start = ((), (), s32[]{:S(2)}) async-start(), calls=%async_computation.9 | async-start | bytes 3538944 | tf_op jit(solution)/shard_map/reduce_scatter | solution.py:101
  128.9 15.1 %slice-start = ((s8[11272192]{0:T(1024)(128)(4,1)}), s8[4194304]{0:T(1024)(128)(4,1)S(1)}, s32[]{:S(2)}) async-start(s8[11272192]{0:T(1024)(128)(4,1)} %bitcast.75), calls=%async_computation.11 | async-start | bytes 8388608
  128.9 15.1 %slice-start.1 = ((s8[11272192]{0:T(1024)(128)(4,1)}), s8[2883584]{0:T(1024)(128)(4,1)S(1)}, s32[]{:S(2)}) async-start(s8[11272192]{0:T(1024)(128)(4,1)} %bitcast.75), calls=%async_computation.12 | async-start | bytes 5767168
  137.8 6.2 %copy-start.10 = (f32[192,1376]{1,0:T(8,128)}, f32[192,1376]{1,0:T(8,128)S(1)}, u32[]{:S(2)}) copy-start(f32[192,1376]{1,0:T(8,128)S(1)} %get-tuple-element.6) | copy-start | bytes 3170308
  137.8 6.2 %slice-start.2 = ((s8[11272192]{0:T(1024)(128)(4,1)}), s8[4194304]{0:T(1024)(128)(4,1)S(1)}, s32[]{:S(2)}) async-start(s8[11272192]{0:T(1024)(128)(4,1)} %bitcast.75), calls=%async_computation.13 | async-start | bytes 8388608
  148.5 1.4 copy-start.7
  157.1 59.4 %copy-start.2 = (bf16[192,4096]{1,0:T(8,128)(2,1)S(1)}, bf16[192,4096]{1,0:T(8,128)(2,1)}, u32[]{:S(2)}) copy-start(bf16[192,4096]{1,0:T(8,128)(2,1)} %all-gather.5.cloned.1.call-done) | copy-start | bytes 4718596
  213.1 77.0 %all-to-all-start.1 = ((bf16[4,6,4096]{2,1,0:T(8,128)(2,1)}), bf16[4,6,4096]{2,1,0:T(8,128)(2,1)S(1)}, u32[]{:S(2)}, u32[]{:S(2)}) async-start(bf16[4,6,4096]{2,1,0:T(8,128)(2,1)} %reshape.136), calls=%async_computation.2 | async-start | bytes 524288 | tf_op jit(solution)/shard_map/all_to_all | solution.py:64
  216.5 83.8 %copy-start.1 = (bf16[16,4096]{1,0:T(8,128)(2,1)S(1)}, bf16[16,4096]{1,0:T(8,128)(2,1)}, u32[]{:S(2)}) copy-start(bf16[16,4096]{1,0:T(8,128)(2,1)} %param.14) | copy-start | bytes 393220
  290.0 9.4 %all-to-all-start.3 = ((bf16[4,6,4096]{2,1,0:T(8,128)(2,1)}), bf16[4,6,4096]{2,1,0:T(8,128)(2,1)S(1)}, u32[]{:S(2)}, u32[]{:S(2)}) async-start(bf16[4,6,4096]{2,1,0:T(8,128)(2,1)} %reshape.139), calls=%async_computation.5 | async-start | bytes 524288 | tf_op jit(solution)/shard_map/all_to_all | solution.py:103
Sparse Core Ops, SparseCore 0:
  20.4 50.1 all-gather.2
  72.7 61.6 all-gather.4
  138.6 72.6 reduce-scatter.2
  214.7 73.4 reduce-scatter.4
